TPU v7x, 8 devices: a whole 2x2x1 slice. The times are simulated.
8 devices in a mesh: data: 1 (over z), outer: 2 (over y), expert: 4 (over x, core).
Axes of the slice: x: 2, y: 2, z: 1, core: 2. Of those that a mesh axis runs over, the one named last changes fastest.
Arguments:
- tokens: bfloat16 [2048, 1536], P(('data', 'outer', 'expert'))
- w_router: bfloat16 [1536, 40], replicated
- routes: int32 [2048, 8], P(('data', 'outer', 'expert'))
- w_gate: bfloat16 [40, 1536, 512], P(('outer', 'expert'))
- w_up: bfloat16 [40, 1536, 512], P(('outer', 'expert'))
- w_down: bfloat16 [40, 512, 1536], P(('outer', 'expert'))
Outputs:
- output: bfloat16 [2048, 1536], P(('data', 'outer', 'expert'))
All inputs are finite; a program needn't handle non-finite values.
Results may differ from a plain program's by a relative error of at most 0.001.
Values are sent between devices in bfloat16 or wider.
A program may use at most 1 GiB of HBM per device.

v0:
```python
import jax
import jax.numpy as jnp
from jax import lax
from jax.sharding import PartitionSpec as P


def local_routes(tokens, w_router, routes, num_dev, capacity):
    tok_count, top_k = routes.shape
    num_exp = w_router.shape[1]
    per_dev = num_exp // num_dev
    logits = jnp.dot(tokens, w_router, preferred_element_type=jnp.float32)
    gate_vals = jax.nn.softmax(jnp.take_along_axis(logits, routes, axis=1), axis=-1)
    flat_ids = routes.reshape(-1)
    onehot = (flat_ids[:, None] == jnp.arange(num_exp)[None, :]).astype(jnp.int32)
    slot_pos = jnp.sum((jnp.cumsum(onehot, axis=0) - onehot) * onehot, axis=1)
    total_slots = num_exp * capacity
    send_pos = (flat_ids % per_dev) * (num_dev * capacity) + (flat_ids // per_dev) * capacity + slot_pos
    dest_slot = jnp.where(slot_pos < capacity, send_pos, total_slots)
    pair_tok = jnp.arange(tok_count * top_k, dtype=jnp.int32) // top_k
    slot_tok = jnp.full((total_slots,), tok_count, jnp.int32).at[dest_slot].set(pair_tok, mode='drop')
    return gate_vals, dest_slot, slot_tok


def expert_ffn(expert_in, w_gate, w_up, w_down):
    gate_act = jnp.einsum('erd,edf->erf', expert_in, w_gate, preferred_element_type=jnp.float32)
    up_lin = jnp.einsum('erd,edf->erf', expert_in, w_up, preferred_element_type=jnp.float32)
    hidden = (jax.nn.silu(gate_act) * up_lin).astype(jnp.bfloat16)
    return jnp.einsum('erf,efd->erd', hidden, w_down, preferred_element_type=jnp.float32).astype(jnp.bfloat16)


def solution(mesh):
    outer_size = mesh.shape['outer']
    group_size = mesh.shape['expert']
    num_dev = outer_size * group_size
    row_spec = P(('data', 'outer', 'expert'), None)
    weight_spec = P(('outer', 'expert'), None, None)

    def per_device(tokens, w_router, routes, w_gate, w_up, w_down):
        tok_count, top_k = routes.shape
        model_dim = tokens.shape[1]
        num_exp = w_router.shape[1]
        per_dev = w_gate.shape[0]
        capacity = (5 * tok_count * top_k + 4 * num_exp - 1) // (4 * num_exp)
        gate_vals, dest_slot, slot_tok = local_routes(tokens, w_router, routes, num_dev, capacity)
        send_buf = jnp.take(tokens, slot_tok, axis=0, mode='fill', fill_value=0)
        send_buf = send_buf.reshape(per_dev, outer_size, group_size, capacity, model_dim)
        recv_buf = lax.all_to_all(send_buf, 'outer', 1, 1, tiled=True)
        recv_buf = lax.all_to_all(recv_buf, 'expert', 2, 2, tiled=True)
        expert_out = expert_ffn(recv_buf.reshape(per_dev, num_dev * capacity, model_dim), w_gate, w_up, w_down)
        back_buf = expert_out.reshape(per_dev, outer_size, group_size, capacity, model_dim)
        back_buf = lax.all_to_all(back_buf, 'expert', 2, 2, tiled=True)
        back_buf = lax.all_to_all(back_buf, 'outer', 1, 1, tiled=True)
        picked = jnp.take(back_buf.reshape(num_exp * capacity, model_dim), dest_slot, axis=0, mode='fill', fill_value=0)
        weighted = gate_vals[:, :, None] * picked.reshape(tok_count, top_k, model_dim).astype(jnp.float32)
        return jnp.sum(weighted, axis=1).astype(jnp.bfloat16)

    return jax.shard_map(per_device, mesh=mesh, in_specs=(row_spec, P(), row_spec, weight_spec, weight_spec, weight_spec), out_specs=row_spec, check_vma=False)
```

profile of v0, /device:TPU:0, one launch (start us, length us, event | category | flops | bytes accessed | tf_op | source)
XLA Modules:
  0.0 488.0 jit_solution(2472724432557127693)
XLA Ops:
  0.0 0.0 copy-start
  0.0 0.9 copy.61
  0.9 0.1 eq.31
  1.0 0.1 eq.27
  1.1 0.7 broadcast_divide_fusion
  1.9 11.3 %reduce-window.6 = s32[40,16,128]{2,1,0:T(8,128)S(1)} reduce-window(s32[40,16,128]{2,1,0:T(8,128)S(1)} %fusion.6, s32[]{:T(128)} %constant.79.clone.1), window={size=1x1x128 pad=0_0x0_0x127_0}, to_apply=%region_2.3 | reduce-window | flops 10403840 | bytes 655364 | tf_op jit(solution)/shard_map/reduce-window
  13.2 0.1 slice.14
  13.4 0.3 copy.78
  13.7 0.2 reduce-window.9
  13.8 0.2 broadcast_add_fusion
  14.0 0.1 fusion.5
  14.2 0.1 reduce_sum.33
  14.3 0.1 copy.65
  14.3 0.7 compare_and_fusion.1
  15.1 0.2 copy.69
  15.2 0.1 ne.72
  15.4 0.1 copy.70
  15.5 0.1 div.42
  15.6 0.1 copy.68
  15.7 0.1 rem.38
  15.9 0.1 compare_select_fusion
  15.9 8.1 %scatter_custom_fusion = s32[2560]{0:T(1024)S(1)} fusion(s32[2048]{0:T(1024)S(1)} %bitcast.50, s32[2048]{0:T(1024)S(1)} %add_select_fusion, s32[]{:T(128)} %constant.92.clone.1), kind=kCustom, calls=%fused_computation.52 | custom fusion | bytes 10244 | tf_op jit(solution)/shard_map/scatter | solution.py:20
  24.0 0.1 broadcast_in_dim.47
  24.1 0.0 copy-done
  24.1 9.5 %gather_fusion = bf16[2560,1536]{1,0:T(8,128)(2,1)} fusion(bf16[256,1536]{1,0:T(8,128)(2,1)S(1)} %copy-done, s32[3072]{0:T(1024)S(1)} %pad_clamp_fusion), kind=kCustom, calls=%fused_computation | custom fusion | bytes 15738880 | tf_op jit(solution)/shard_map/jit(_take)/gather | solution.py:45
  33.7 4.7 copy_select_fusion
  38.3 92.8 %all_to_all.20 = bf16[5,2,4,64,1536]{4,3,2,0,1:T(8,128)(2,1)} all-to-all(bf16[5,2,4,64,1536]{4,3,2,0,1:T(8,128)(2,1)S(1)} %copy_select_fusion), channel_id=1, replica_groups=mesh['data'=1,'outer'=2,'expert'=4] {'outer'}, dimensions={1} | all-to-all | bytes 15728640 | tf_op jit(solution)/shard_map/all_to_all | solution.py:47
  131.1 3.7 copy.73
  134.8 91.1 %all_to_all.21 = bf16[5,2,4,64,1536]{4,3,1,0,2:T(8,128)(2,1)} all-to-all(bf16[5,2,4,64,1536]{4,3,1,0,2:T(8,128)(2,1)S(1)} %copy.73), channel_id=1, replica_groups=mesh['data'=1,'outer'=2,'expert'=4] {'expert'}, dimensions={2} | all-to-all | bytes 15728640 | tf_op jit(solution)/shard_map/all_to_all | solution.py:48
  225.9 3.7 copy.74
  229.7 0.0 copy-start.1
  229.7 3.1 copy-done.1
  232.7 9.2 %fusion.25 = f32[5,512,512]{2,1,0:T(8,128)} fusion(bf16[5,512,1536]{2,1,0:T(8,128)(2,1)S(1)} %bitcast.43, bf16[5,1536,512]{2,1,0:T(8,128)(2,1)} %param.9), kind=kOutput, calls=%fused_computation.60 | convolution fusion | flops 4026531840 | bytes 20971520 | tf_op jit(solution)/shard_map/erd,edf->erf/dot_general | solution.py:25
  241.9 18.0 %convolution_convert_fusion = bf16[5,512,1536]{2,1,0:T(8,128)(2,1)} fusion(bf16[5,512,1536]{2,1,0:T(8,128)(2,1)} %param.11, f32[5,512,512]{2,1,0:T(8,128)} %fusion.25, bf16[5,512,1536]{2,1,0:T(8,128)(2,1)} %bitcast.44, bf16[5,1536,512]{2,1,0:T(8,128)(2,1)} %param.10), kind=kOutput, calls=%fused_computation.7 | convolution fusion | flops 8064860160 | bytes 36700160 | tf_op jit(solution)/shard_map/erf,efd->erd/dot_general | solution.py:28
  259.9 3.7 copy.75
  263.6 91.1 %all_to_all.22 = bf16[5,2,4,64,1536]{4,3,1,0,2:T(8,128)(2,1)} all-to-all(bf16[5,2,4,64,1536]{4,3,1,0,2:T(8,128)(2,1)S(1)} %copy.75), channel_id=1, replica_groups=mesh['data'=1,'outer'=2,'expert'=4] {'expert'}, dimensions={2} | all-to-all | bytes 15728640 | tf_op jit(solution)/shard_map/all_to_all | solution.py:51
  354.7 7.3 %copy.76 = bf16[5,2,4,64,1536]{4,3,2,0,1:T(8,128)(2,1)} copy(bf16[5,2,4,64,1536]{4,3,1,0,2:T(8,128)(2,1)} %all_to_all.22) | data formatting | bytes 15728640 | tf_op jit(solution)/shard_map/all_to_all | solution.py:51
  362.0 0.0 copy-start.2
  362.0 0.0 copy-start.3
  362.0 6.9 %all-to-all-start.3 = ((bf16[5,2,4,64,1536]{4,3,2,0,1:T(8,128)(2,1)}), bf16[5,2,4,64,1536]{4,3,2,0,1:T(8,128)(2,1)}, u32[]{:S(2)}, u32[]{:S(2)}) async-start(bf16[5,2,4,64,1536]{4,3,2,0,1:T(8,128)(2,1)} %copy.76), calls=%async_computation.3 | async-start | bytes 15728640 | tf_op jit(solution)/shard_map/all_to_all | solution.py:52
  368.9 0.0 copy-done.2
  368.9 0.1 copy.58
  369.1 0.1 reshape.196
  369.2 0.0 copy-done.3
  369.2 0.3 fusion.24
  369.5 16.8 %gather_fusion.2 = f32[2048]{0:T(1024)S(1)} fusion(f32[256,40]{0,1:T(8,128)S(1)} %fusion.24, s32[2048]{0:T(1024)S(1)} %reshape.196), kind=kCustom, calls=%fused_computation.2 | custom fusion | bytes 32768 | tf_op jit(solution)/shard_map/jit(take_along_axis)/gather | solution.py:12
  386.3 0.1 reshape.199
  386.4 0.1 copy.59
  386.6 0.1 copy.60
  386.7 0.2 copy.67
  386.9 68.3 %all-to-all-done.3 = bf16[5,2,4,64,1536]{4,3,2,0,1:T(8,128)(2,1)} async-done(((bf16[5,2,4,64,1536]{4,3,2,0,1:T(8,128)(2,1)}), bf16[5,2,4,64,1536]{4,3,2,0,1:T(8,128)(2,1)}, u32[]{:S(2)}, u32[]{:S(2)}) %all-to-all-start.3) | async-done | bytes 7864352 | tf_op jit(solution)/shard_map/all_to_all | solution.py:52
  455.2 7.3 %copy.77 = bf16[5,2,4,64,1536]{4,3,2,1,0:T(8,128)(2,1)} copy(bf16[5,2,4,64,1536]{4,3,2,0,1:T(8,128)(2,1)} %all-to-all-done.3) | data formatting | bytes 15728640 | tf_op jit(solution)/shard_map/all_to_all | solution.py:52
  462.5 17.5 %gather_fusion.1 = bf16[2048,1536]{1,0:T(8,128)(2,1)} fusion(bf16[2560,1536]{1,0:T(8,128)(2,1)} %bitcast.41, s32[2048]{0:T(1024)S(1)} %broadcast_clamp_fusion), kind=kCustom, calls=%fused_computation.1 | custom fusion | bytes 12591104 | tf_op jit(solution)/shard_map/jit(_take)/gather | solution.py:53
  480.0 8.1 %multiply_reduce_fusion = bf16[256,1536]{1,0:T(8,128)(2,1)} fusion(bf16[2048,1536]{1,0:T(8,128)(2,1)} %gather_fusion.1, f32[256,8]{1,0:T(8,128)S(1)} %copy.60, pred[256,8]{1,0:T(8,128)(4,1)S(1)} %copy.67), kind=kLoop, calls=%fused_computation.4 | loop fusion | flops 12189696 | bytes 7088128 | tf_op jit(solution)/shard_map/reduce_sum | solution.py:55
  (10 shorter events, 0.1 us)
Async XLA Ops:
  0.0 24.1 %copy-start = (bf16[256,1536]{1,0:T(8,128)(2,1)S(1)}, bf16[256,1536]{1,0:T(8,128)(2,1)}, u32[]{:S(2)}) copy-start(bf16[256,1536]{1,0:T(8,128)(2,1)} %param.6) | copy-start | bytes 2359300
  229.7 3.1 copy-start.1
  362.0 6.9 %copy-start.2 = (s32[256,8]{0,1:T(8,128)S(1)}, s32[256,8]{0,1:T(8,128)}, u32[]{:S(2)}) copy-start(s32[256,8]{0,1:T(8,128)} %param.8) | copy-start | bytes 24580
  362.0 7.2 %copy-start.3 = (bf16[1536,40]{0,1:T(8,128)(2,1)S(1)}, bf16[1536,40]{0,1:T(8,128)(2,1)}, u32[]{:S(2)}) copy-start(bf16[1536,40]{0,1:T(8,128)(2,1)} %param.7) | copy-start | bytes 368644
  362.0 93.2 %all-to-all-start.3 = ((bf16[5,2,4,64,1536]{4,3,2,0,1:T(8,128)(2,1)}), bf16[5,2,4,64,1536]{4,3,2,0,1:T(8,128)(2,1)}, u32[]{:S(2)}, u32[]{:S(2)}) async-start(bf16[5,2,4,64,1536]{4,3,2,0,1:T(8,128)(2,1)} %copy.76), calls=%async_computation.3 | async-start | bytes 15728640 | tf_op jit(solution)/shard_map/all_to_all | solution.py:52
where the time goes:
time: 489 us; the launch traced here: 488 us
  blocking collectives  275 us (56%)
  local copies, waits for them, and re-layouts  84 us (17%)
  waiting for transfers between devices  68.3 us (14%)
  matrix products  27.5 us (6%)
  other arithmetic  26.2 us (5%)
  starting transfers between devices  6.91 us (1%)
    all_to_all x1, blocking collectives, per_device(): recv_buf = lax.all_to_all(send_buf, 'outer', 1, 1, tiled=True)  92.8 us
    all_to_all x1, blocking collectives, per_device(): back_buf = lax.all_to_all(back_buf, 'expert', 2, 2, tiled=True)  91.1 us
    all_to_all x1, blocking collectives, per_device(): recv_buf = lax.all_to_all(recv_buf, 'expert', 2, 2, tiled=True)  91.1 us
    all_to_all x1, waiting for transfers between devices, per_device(): back_buf = lax.all_to_all(back_buf, 'outer', 1, 1, tiled=True)  68.3 us
    dot_general x1, matrix products, expert_ffn(): jnp.einsum('erf,efd->erd', hidden, w_down, preferred_element_type=jnp.flo...  18 us
    gather x1, local copies, waits for them, and re-layouts, per_device(): jnp.take(back_buf.reshape(num_exp * capacity, model_dim), dest_slot, axis...  17.5 us
    gather x5, local copies, waits for them, and re-layouts, local_routes(): jnp.take_along_axis(logits, routes, axis=1)  17.2 us
    another operation x3, other arithmetic  11.7 us
  transfers between devices with their start and end apart: 1, of which 1 were waited for; matrix products, arithmetic and copies ran while one was open for 4% of the time, Pallas kernels for 0%

commit v1 on v0

v1 whole, which is shorter than its diff:
```python
import jax
import jax.numpy as jnp
from jax import lax
from jax.experimental import pallas as pl
from jax.experimental.pallas import tpu as pltpu
from jax.sharding import PartitionSpec as P

MESH = pl.DeviceIdType.MESH
BF16 = jnp.bfloat16
F32 = jnp.float32
LANES = 128


def local_routes(tokens, w_router, routes, num_dev, capacity):
    tok_count, top_k = routes.shape
    num_exp = w_router.shape[1]
    per_dev = num_exp // num_dev
    logits = jnp.dot(tokens, w_router, preferred_element_type=jnp.float32)
    gate_vals = jax.nn.softmax(jnp.take_along_axis(logits, routes, axis=1), axis=-1)
    flat_ids = routes.reshape(-1)
    onehot = (flat_ids[:, None] == jnp.arange(num_exp)[None, :]).astype(jnp.int32)
    slot_pos = jnp.sum((jnp.cumsum(onehot, axis=0) - onehot) * onehot, axis=1)
    total_slots = num_exp * capacity
    send_pos = (flat_ids % per_dev) * (num_dev * capacity) + (flat_ids // per_dev) * capacity + slot_pos
    dest_slot = jnp.where(slot_pos < capacity, send_pos, total_slots)
    pair_tok = jnp.arange(tok_count * top_k, dtype=jnp.int32) // top_k
    slot_tok = jnp.full((total_slots,), tok_count, jnp.int32).at[dest_slot].set(pair_tok, mode='drop')
    return gate_vals, dest_slot, slot_tok


def expert_ffn(expert_in, w_gate, w_up, w_down):
    gate_act = jnp.einsum('erd,edf->erf', expert_in, w_gate, preferred_element_type=jnp.float32)
    up_lin = jnp.einsum('erd,edf->erf', expert_in, w_up, preferred_element_type=jnp.float32)
    hidden = (jax.nn.silu(gate_act) * up_lin).astype(jnp.bfloat16)
    return jnp.einsum('erf,efd->erd', hidden, w_down, preferred_element_type=jnp.float32).astype(jnp.bfloat16)


def plain_layer(tokens, w_router, routes, w_gate, w_up, w_down, outer_size, group_size, capacity):
    num_dev = outer_size * group_size
    tok_count, top_k = routes.shape
    model_dim = tokens.shape[1]
    num_exp = w_router.shape[1]
    per_dev = w_gate.shape[0]
    gate_vals, dest_slot, slot_tok = local_routes(tokens, w_router, routes, num_dev, capacity)
    send_buf = jnp.take(tokens, slot_tok, axis=0, mode='fill', fill_value=0)
    send_buf = send_buf.reshape(per_dev, outer_size, group_size, capacity, model_dim)
    recv_buf = lax.all_to_all(send_buf, 'outer', 1, 1, tiled=True)
    recv_buf = lax.all_to_all(recv_buf, 'expert', 2, 2, tiled=True)
    expert_out = expert_ffn(recv_buf.reshape(per_dev, num_dev * capacity, model_dim), w_gate, w_up, w_down)
    back_buf = expert_out.reshape(per_dev, outer_size, group_size, capacity, model_dim)
    back_buf = lax.all_to_all(back_buf, 'expert', 2, 2, tiled=True)
    back_buf = lax.all_to_all(back_buf, 'outer', 1, 1, tiled=True)
    picked = jnp.take(back_buf.reshape(num_exp * capacity, model_dim), dest_slot, axis=0, mode='fill', fill_value=0)
    weighted = gate_vals[:, :, None] * picked.reshape(tok_count, top_k, model_dim).astype(jnp.float32)
    return jnp.sum(weighted, axis=1).astype(jnp.bfloat16)


ROWS_CAP = 192
CHUNKS = 4
NBLK = 512
GATE_ROWS = 40
META_ROWS = 88


def moe_kernel(capacity, tok_hbm, routes_ref, wr_ref, wg_hbm, wu_hbm, wd_hbm, out_ref, flag_ref,
               X, M, Wg, Wu, Wd, Xs, Ob, Pt, Rd, Rx, TL, TS, TR, Lg, Kc,
               tok_send, tok_recv, meta_send, meta_recv, d_send, d_recv, x_send, x_recv, y_send, y_recv, w_sem, loc_sem):
    data = lax.axis_index('data')
    o = lax.axis_index('outer')
    e = lax.axis_index('expert')
    x = e // 2
    c = e % 2
    me = o * 4 + e
    num_tok, dim = tok_hbm.shape
    num_exp = wr_ref.shape[1]
    per_dev = wg_hbm.shape[0]
    cap = ROWS_CAP
    ck_rows = cap // CHUNKS
    id_p = (data, o, x * 2 + 1 - c)
    id_x = (data, o, (1 - x) * 2 + c)
    id_y = (data, 1 - o, e)

    def home(dy, dx, hc):
        return lax.rem(o + dy, 2) * 4 + lax.rem(x + dx, 2) * 2 + hc

    h_x, h_y, h_d = home(0, 1, c), home(1, 0, c), home(1, 1, c)

    barrier = pltpu.get_barrier_semaphore()
    for dev in (id_p, id_x, id_y):
        pl.semaphore_signal(barrier, inc=1, device_id=dev, device_id_type=MESH)
    pl.semaphore_wait(barrier, 3)

    def tok_copy(slot, h, dev, own=False):
        return pltpu.make_async_remote_copy(
            src_ref=tok_hbm if own else X.at[h], dst_ref=X.at[h], send_sem=tok_send.at[slot],
            recv_sem=tok_recv.at[h], device_id=dev, device_id_type=MESH)

    def meta_copy(slot, h, dev):
        return pltpu.make_async_remote_copy(
            src_ref=M.at[h], dst_ref=M.at[h], send_sem=meta_send.at[slot],
            recv_sem=meta_recv.at[h], device_id=dev, device_id_type=MESH)

    load_tok = pltpu.make_async_copy(tok_hbm, X.at[me], loc_sem.at[0])
    load_tok.start()
    sends = [(0, me, id_x), (1, me, id_y), (2, me, id_p), (3, h_x, id_y), (4, h_x, id_p), (5, h_y, id_p), (6, h_d, id_p)]
    for slot, h, dev in sends[:3]:
        tok_copy(slot, h, dev, own=True).start()

    def weight_copies(j):
        return [pltpu.make_async_copy(src.at[j], dst.at[j], w_sem.at[k, j])
                for k, (src, dst) in enumerate(((wg_hbm, Wg), (wu_hbm, Wu), (wd_hbm, Wd)))]

    for j in range(per_dev):
        for cp in weight_copies(j):
            cp.start()

    load_tok.wait()
    Lg[...] = jnp.zeros_like(Lg)
    Lg[:, 0:num_exp] = jnp.dot(X[me], wr_ref[...], preferred_element_type=F32)
    logits = Lg[...]
    lane = lax.broadcasted_iota(jnp.int32, (num_tok, LANES), 1)
    routes = routes_ref[...]
    routed = lane == routes[:, 0:1]
    for j in range(1, routes.shape[1]):
        routed = jnp.logical_or(routed, lane == routes[:, j:j + 1])
    top = jnp.max(jnp.where(routed, logits, -jnp.inf), axis=1, keepdims=True)
    ex = jnp.where(routed, jnp.exp(jnp.where(routed, logits - top, 0.0)), 0.0)
    gates = ex / jnp.sum(ex, axis=1, keepdims=True)
    routed_f = jnp.where(routed, 1.0, 0.0)
    upper = jnp.max(jnp.where(lane >= num_exp // 2, routed_f, 0.0), axis=1, keepdims=True)
    marks = routed_f + jnp.where(lane == num_exp, 1.0 - upper, 0.0) + jnp.where(lane == num_exp + 1, upper, 0.0)
    earlier = (lax.broadcasted_iota(jnp.int32, (num_tok, num_tok), 1) < lax.broadcasted_iota(jnp.int32, (num_tok, num_tok), 0))
    before = jnp.dot(jnp.where(earlier, 1.0, 0.0).astype(BF16), marks.astype(BF16), preferred_element_type=F32)
    kept = jnp.logical_and(marks > 0.5, jnp.logical_or(lane >= num_exp, before < capacity))
    rank = jnp.where(kept, before, -1.0)
    n_up = jnp.sum(upper, axis=0, keepdims=True)
    over = jnp.where(jnp.maximum(n_up, num_tok - n_up) > cap, 1.0, 0.0)
    rank = jnp.where(lane == num_exp + 2, over, rank)
    Kc[...] = rank
    gates = jnp.where(kept, gates, 0.0)
    M[me, 0:GATE_ROWS, :] = jnp.transpose(gates)[0:GATE_ROWS]
    M[me, GATE_ROWS:META_ROWS, :] = jnp.transpose(rank)[0:META_ROWS - GATE_ROWS]
    for slot, h, dev in sends[:3]:
        meta_copy(slot, h, dev).start()

    slot_iota = lax.broadcasted_iota(jnp.int32, (capacity, num_tok), 0).astype(F32)
    rank_iota = lax.broadcasted_iota(jnp.int32, (cap, num_tok), 0).astype(F32)

    def fill(h, hc):
        parts = []
        for j in range(per_dev):
            pos = M[h, pl.ds(GATE_ROWS + me * per_dev + j, 1), :]
            parts.append(jnp.where(pos == slot_iota, 1.0, 0.0).astype(BF16))
        pick = jnp.concatenate(parts, axis=0)
        for n in range(0, dim, NBLK):
            rows = jnp.dot(pick, X[h, :, n:n + NBLK], preferred_element_type=F32).astype(BF16)
            for j in range(per_dev):
                Xs[j, hc * capacity:(hc + 1) * capacity, n:n + NBLK] = rows[j * capacity:(j + 1) * capacity]

    def combine(h, hc):
        parts = []
        for j in range(per_dev):
            pos = M[h, pl.ds(GATE_ROWS + me * per_dev + j, 1), :]
            gate = M[h, pl.ds(me * per_dev + j, 1), :]
            parts.append(jnp.where(pos == slot_iota, gate, 0.0))
        spread = jnp.concatenate(parts, axis=0)
        where_to = jnp.where(M[h, pl.ds(GATE_ROWS + num_exp + o, 1), :] == rank_iota, 1.0, 0.0).astype(BF16)
        weights = []
        for _ in range(3):
            part = spread.astype(BF16)
            spread = spread - part.astype(F32)
            weights.append(lax.dot_general(where_to, part, (((1,), (1,)), ((), ())), preferred_element_type=F32).astype(BF16))
        for n in range(0, dim, NBLK):
            outs = Ob[hc, :, n:n + NBLK]
            acc = jnp.dot(weights[0], outs, preferred_element_type=F32)
            acc += jnp.dot(weights[1], outs, preferred_element_type=F32)
            acc += jnp.dot(weights[2], outs, preferred_element_type=F32)
            Pt[h, :, n:n + NBLK] = acc

    def d_copy(chip):
        return pltpu.make_async_remote_copy(
            src_ref=Pt.at[chip * 2 + 1 - c], dst_ref=Rd.at[chip], send_sem=d_send.at[chip], recv_sem=d_recv.at[chip],
            device_id=id_p, device_id_type=MESH)

    def x_copy(chip, ho, k):
        rows = pl.ds(k * ck_rows, ck_rows)
        return pltpu.make_async_remote_copy(
            src_ref=Pt.at[chip * 2 + c, rows], dst_ref=Rx.at[ho, rows], send_sem=x_send.at[ho, k], recv_sem=x_recv.at[ho, k],
            device_id=id_x, device_id_type=MESH)

    def y_copy(k):
        rows = pl.ds(k * ck_rows, ck_rows)
        return pltpu.make_async_remote_copy(
            src_ref=TS.at[rows], dst_ref=TR.at[rows], send_sem=y_send.at[k], recv_sem=y_recv.at[k],
            device_id=id_y, device_id_type=MESH)

    def arrived(h):
        tok_copy(0, h, id_p).wait_recv()
        meta_copy(0, h, id_p).wait_recv()

    def forward(which):
        slot, h, dev = sends[which]
        tok_copy(slot, h, dev).start()
        meta_copy(slot, h, dev).start()

    def group(g, carry):
        hx, ho = lax.rem(x + lax.rem(g, 2), 2), lax.rem(o + g // 2, 2)
        chip = ho * 2 + hx

        @pl.when(g == 1)
        def _():
            arrived(h_x)
            forward(3)
            forward(4)
            arrived(h_y)
            forward(5)

        @pl.when(g == 3)
        def _():
            arrived(h_d)
            forward(6)

        arrived(chip * 2 + 1 - c)
        for hc in range(2):
            fill(chip * 2 + hc, hc)

        def expert(j, carry):
            @pl.when(g == 0)
            def _():
                for cp in weight_copies(j):
                    cp.wait()

            rows = Xs[j]
            act = jnp.dot(rows, Wg[j], preferred_element_type=F32)
            lin = jnp.dot(rows, Wu[j], preferred_element_type=F32)
            hidden = (jax.nn.silu(act) * lin).astype(BF16)
            for n in range(0, dim, NBLK):
                res = jnp.dot(hidden, Wd[j, :, n:n + NBLK], preferred_element_type=F32).astype(BF16)
                for hc in range(2):
                    Ob[hc, pl.ds(pl.multiple_of(j * capacity, capacity), capacity), n:n + NBLK] = res[hc * capacity:(hc + 1) * capacity]
            return carry

        lax.fori_loop(0, per_dev, expert, 0)
        for hc in range(2):
            combine(chip * 2 + hc, hc)
        d_copy(chip).start()
        d_copy(chip).wait_recv()
        for k in range(CHUNKS):
            rows = pl.ds(k * ck_rows, ck_rows)
            Pt[chip * 2 + c, rows, :] = Pt[chip * 2 + c, rows, :] + Rd[chip, rows, :]

            @pl.when(lax.rem(g, 2) == 1)
            def _():
                x_copy(chip, ho, k).start()
        return carry

    lax.fori_loop(0, 4, group, 0)

    own = me
    for k in range(CHUNKS):
        rows = pl.ds(k * ck_rows, ck_rows)
        x_copy(0, o, k).wait_recv()
        TL[rows, :] = (Pt[own, rows, :] + Rx[o, rows, :]).astype(BF16)
    for k in range(CHUNKS):
        rows = pl.ds(k * ck_rows, ck_rows)
        x_copy(0, 1 - o, k).wait_recv()
        TS[rows, :] = (Pt[h_y, rows, :] + Rx[1 - o, rows, :]).astype(BF16)
        y_copy(k).start()

    over_all = M[0, GATE_ROWS + num_exp + 2:GATE_ROWS + num_exp + 3, :]
    for h in range(1, 8):
        over_all = jnp.maximum(over_all, M[h, GATE_ROWS + num_exp + 2:GATE_ROWS + num_exp + 3, :])
    flag_ref[...] = jnp.broadcast_to(jnp.max(over_all, axis=1, keepdims=True), flag_ref.shape)

    cap_iota = lax.broadcasted_iota(jnp.int32, (num_tok, cap), 1).astype(F32)
    rank_0, rank_1 = Kc[:, num_exp:num_exp + 1], Kc[:, num_exp + 1:num_exp + 2]
    here = jnp.where(o == 0, rank_0, rank_1)
    there = jnp.where(o == 0, rank_1, rank_0)
    take_here = jnp.where(here == cap_iota, 1.0, 0.0).astype(BF16)
    take_there = jnp.where(there == cap_iota, 1.0, 0.0).astype(BF16)
    for k in range(CHUNKS):
        y_copy(k).wait_recv()
    for n in range(0, dim, NBLK):
        acc = jnp.dot(take_here, TL[:, n:n + NBLK], preferred_element_type=F32)
        acc += jnp.dot(take_there, TR[:, n:n + NBLK], preferred_element_type=F32)
        out_ref[:, n:n + NBLK] = acc.astype(BF16)

    for slot, h, dev in sends:
        tok_copy(slot, h, dev).wait_send()
        meta_copy(slot, h, dev).wait_send()
    for chip in range(4):
        d_copy(chip).wait_send()
    for k in range(CHUNKS):
        for ho in range(2):
            x_copy(0, ho, k).wait_send()
        y_copy(k).wait_send()


def solution(mesh):
    outer_size = mesh.shape['outer']
    group_size = mesh.shape['expert']
    row_spec = P(('data', 'outer', 'expert'), None)
    weight_spec = P(('outer', 'expert'), None, None)

    def per_device(tokens, w_router, routes, w_gate, w_up, w_down):
        tok_count, top_k = routes.shape
        dim = tokens.shape[1]
        num_exp = w_router.shape[1]
        per_dev, _, ffn = w_gate.shape
        capacity = (5 * tok_count * top_k + 4 * num_exp - 1) // (4 * num_exp)
        homes = outer_size * group_size
        cap = ROWS_CAP
        vmem = pl.BlockSpec(memory_space=pltpu.VMEM)
        hbm = pl.BlockSpec(memory_space=pl.ANY)
        dma = pltpu.SemaphoreType.DMA

        def body(*refs):
            moe_kernel(capacity, *refs)

        fast, flag = pl.pallas_call(
            body,
            out_shape=(jax.ShapeDtypeStruct((tok_count, dim), BF16), jax.ShapeDtypeStruct((8, LANES), F32)),
            in_specs=[hbm, vmem, vmem, hbm, hbm, hbm],
            out_specs=(vmem, vmem),
            scratch_shapes=[
                pltpu.VMEM((homes, tok_count, dim), BF16),
                pltpu.VMEM((homes, META_ROWS, tok_count), F32),
                pltpu.VMEM((per_dev, dim, ffn), BF16),
                pltpu.VMEM((per_dev, dim, ffn), BF16),
                pltpu.VMEM((per_dev, ffn, dim), BF16),
                pltpu.VMEM((per_dev, 2 * capacity, dim), BF16),
                pltpu.VMEM((2, per_dev * capacity, dim), BF16),
                pltpu.VMEM((homes, cap, dim), F32),
                pltpu.VMEM((homes // 2, cap, dim), F32),
                pltpu.VMEM((2, cap, dim), F32),
                pltpu.VMEM((cap, dim), BF16),
                pltpu.VMEM((cap, dim), BF16),
                pltpu.VMEM((cap, dim), BF16),
                pltpu.VMEM((tok_count, LANES), F32),
                pltpu.VMEM((tok_count, LANES), F32),
                dma((7,)), dma((homes,)), dma((7,)), dma((homes,)),
                dma((4,)), dma((4,)),
                dma((2, CHUNKS)), dma((2, CHUNKS)), dma((CHUNKS,)), dma((CHUNKS,)),
                dma((3, per_dev)), dma((1,)),
            ],
            compiler_params=pltpu.CompilerParams(collective_id=0, has_side_effects=True, vmem_limit_bytes=66_000_000),
            name='moe',
        )(tokens, routes, w_router, w_gate, w_up, w_down)

        def slow():
            return plain_layer(tokens, w_router, routes, w_gate, w_up, w_down, outer_size, group_size, capacity)

        return lax.cond(flag[0, 0] > 0.5, slow, lambda: fast)

    return jax.shard_map(per_device, mesh=mesh, in_specs=(row_spec, P(), row_spec, weight_spec, weight_spec, weight_spec), out_specs=row_spec, check_vma=False)
```

time: 489 us -> 103 us (0.21)
  blocking collectives: 275 us -> 0 us
  Pallas kernels: 0 us -> 95.3 us
  local copies, waits for them, and re-layouts: 84 us -> 6.55 us
  waiting for transfers between devices: 68.3 us -> 0 us
  matrix products: 27.5 us -> 0 us
  other arithmetic: 26.2 us -> 0 us
  starting transfers between devices: 6.91 us -> 0 us
    all_to_all x3 -> x0, blocking collectives: 275 us -> none  [the longest x1 92.8 us: per_device(): recv_buf = lax.all_to_all(send_buf, 'outer', 1, 1, tiled=True)]
    pallas_call x0 -> x1, Pallas kernels: none -> 95.3 us  [per_device(): pl.pallas_call(body, out_shape=(jax.ShapeDtypeStruct((tok_count, dim), BF...]
    all_to_all x1 -> x0, waiting for transfers between devices: 68.3 us -> none  [per_device(): back_buf = lax.all_to_all(back_buf, 'outer', 1, 1, tiled=True)]
    gather x7 -> x0, local copies, waits for them, and re-layouts: 44.2 us -> none  [the longest x1 17.5 us: per_device(): jnp.take(back_buf.reshape(num_exp * capacity, model_dim), dest_slot, axis...]
    dot_general x3 -> x0, matrix products: 27.5 us -> none  [the longest x1 18 us: expert_ffn(): jnp.einsum('erf,efd->erd', hidden, w_down, preferred_element_type=jnp.flo...]
    all_to_all x4 -> x0, local copies, waits for them, and re-layouts: 22 us -> none  [the longest x1 7.28 us: per_device(): back_buf = lax.all_to_all(back_buf, 'expert', 2, 2, tiled=True)]
    another operation x3 -> x0, other arithmetic: 11.7 us -> none
    reduce_sum x3 -> x0, other arithmetic: 8.23 us -> none  [the longest x1 8.05 us: per_device(): return jnp.sum(weighted, axis=1).astype(jnp.bfloat16)]
  transfers between devices with their start and end apart: 1 -> 0, of which waited for: 1 -> 0; matrix products, arithmetic and copies ran while one was open for 4% -> 0% of each run, Pallas kernels for 0% -> 0%
where the time goes in v1:
time: 103 us
  Pallas kernels  95.3 us (93%)
  local copies, waits for them, and re-layouts  6.55 us (6%)
    pallas_call x1, Pallas kernels, per_device(): pl.pallas_call(body, out_shape=(jax.ShapeDtypeStruct((tok_count, dim), BF...  95.3 us
    unnamed x9, local copies, waits for them, and re-layouts  5.36 us

profile of v1, /device:TPU:0, one launch (start us, length us, event | category | flops | bytes accessed | tf_op | source)
XLA Modules:
  0.0 102.8 jit_solution(15367888690013036253)
XLA Ops:
  0.0 1.5 %copy.40.refs_1_ = s32[256,8]{1,0:T(8,128)} copy(s32[256,8]{0,1:T(8,128)} %param.10) | data formatting | bytes 16384 | tf_op args[2]
  1.5 1.8 %copy.41.refs_2_ = bf16[1536,40]{1,0:T(8,128)(2,1)} copy(bf16[1536,40]{0,1:T(8,128)(2,1)} %param.9) | data formatting | bytes 245760 | tf_op args[1]
  3.3 0.0 copy-start
  3.3 0.0 copy-start.2
  3.3 0.0 copy-start.3
  3.3 95.3 %moe.1 = (bf16[256,1536]{1,0:T(8,128)(2,1)}, f32[8,128]{1,0:T(8,128)}) custom-call(bf16[256,1536]{1,0:T(8,128)(2,1)} %refs_0_.1, s32[256,8]{1,0:T(8,128)} %copy.40.refs_1_, bf16[1536,40]{1,0:T(8,128)(2,1)} %copy.41.refs_2_, bf16[5,1536,512]{2,1,0:T(8,128)(2,1)} %refs_3_.1, bf16[5,1536,512]{2,1,0:T(8,128)(2,1)} %refs_4_.1, bf16[5,512,1536]{2,1,0:T(8,128)(2,1)} %refs_5_.1), custom_call_target="tpu_custom_call" | custom-call | tf_op jit(solution)/shard_map/moe/pallas_call | solution.py:320
  98.6 1.2 %slice.9 = f32[1,1]{1,0:T(1,128)} slice(f32[8,128]{1,0:T(8,128)} %get-tuple-element.29), slice={[0:1], [0:1]} | slice | bytes 8 | tf_op jit(solution)/shard_map/slice | solution.py:353
  100.5 0.0 copy-done
  100.5 0.0 copy-done.2
  100.5 0.0 copy-done.3
  100.5 0.2 conditional.1
  100.7 2.1 %copy.54 = bf16[256,1536]{1,0:T(8,128)(2,1)} copy(bf16[256,1536]{1,0:T(8,128)(2,1)} %get-tuple-element.31) | data formatting | bytes 1572864
Async XLA Ops:
  3.3 97.2 %copy-start = (bf16[256,1536]{1,0:T(8,128)(2,1)S(1)}, bf16[256,1536]{1,0:T(8,128)(2,1)}, u32[]{:S(2)}) copy-start(bf16[256,1536]{1,0:T(8,128)(2,1)} %refs_0_.1) | copy-start | bytes 2359300
  3.3 97.2 %copy-start.2 = (bf16[1536,40]{0,1:T(8,128)(2,1)S(1)}, bf16[1536,40]{0,1:T(8,128)(2,1)}, u32[]{:S(2)}) copy-start(bf16[1536,40]{0,1:T(8,128)(2,1)} %param.9) | copy-start | bytes 368644
  3.3 97.2 %copy-start.3 = (s32[256,8]{0,1:T(8,128)S(1)}, s32[256,8]{0,1:T(8,128)}, u32[]{:S(2)}) copy-start(s32[256,8]{0,1:T(8,128)} %param.10) | copy-start | bytes 24580
